TPU v7x, 32 devices: a whole 2x2x4 slice. The times are simulated.
32 devices in a mesh: row: 8 (over y, x, core), col: 4 (over z).
Axes of the slice: x: 2, y: 2, z: 4, core: 2. Of those that a mesh axis runs over, the one named last changes fastest.
Arguments:
- pair_state: bfloat16 [128, 128, 128], P('row', 'col'), may hold values from -6 to 6
- pair_mask: int32 [128, 128], P('row', 'col'), may hold values 0 or 1
- input_gain: float32 [2, 128], replicated, may hold values from 0.25 to 1.75
- input_bias: float32 [2, 128], replicated, may hold values from -1.5 to 1.5
- proj_weights: bfloat16 [2, 128, 512], replicated, may hold values from -0.5 to 0.5
- gate_weights: bfloat16 [2, 128, 128], replicated, may hold values from -0.5 to 0.5
- output_gain: float32 [2, 128], replicated, may hold values from 0.25 to 1.75
- output_bias: float32 [2, 128], replicated, may hold values from -1.5 to 1.5
- output_weights: bfloat16 [2, 128, 128], replicated, may hold values from -0.5 to 0.5
Outputs:
- pair_out: bfloat16 [128, 128, 128], P('row', 'col')
All inputs are finite; a program needn't handle non-finite values. No bound on the sum of `pair_mask` on one device may be relied on, other than what follows from the above.
Results may differ from a plain program's by a relative error of at most 0.0058.
Values may be sent and summed in bfloat16 or wider, within the bound.
A program may use at most 64 MiB of HBM per device.

v0:
```python
import functools

import jax
import jax.numpy as jnp
from jax import lax
from jax.experimental import pallas as pl
from jax.experimental.pallas import tpu as pltpu
from jax.sharding import PartitionSpec as P

epsilon = 1e-05


def normalize(values, weight_scale, weight_shift, reduce_axis):
    average = jnp.mean(values, axis=reduce_axis, keepdims=True)
    centred = values - average
    spread = jnp.mean(centred * centred, axis=reduce_axis, keepdims=True)
    return centred * lax.rsqrt(spread + epsilon) * weight_scale + weight_shift


def contract(left_panel, right_panel, layer_index):
    if layer_index == 0:
        product = jnp.einsum(
            "cik,cjk->cij", left_panel, right_panel, preferred_element_type=jnp.float32
        )
    else:
        product = jnp.einsum(
            "cki,ckj->cij", left_panel, right_panel, preferred_element_type=jnp.float32
        )
    return product.astype(jnp.bfloat16)


def gated_panel(pair_ln, weights, first, hidden, mask_float):
    projected = jnp.einsum(
        "ijd,de->eij",
        pair_ln,
        weights[:, first : first + 2 * hidden],
        preferred_element_type=jnp.float32,
    )
    return (jax.nn.sigmoid(projected[:hidden]) * projected[hidden:] * mask_float).astype(
        jnp.bfloat16
    )


def on_device(
    pair_state,
    pair_mask,
    input_gain,
    input_bias,
    proj_weights,
    gate_weights,
    output_gain,
    output_bias,
    output_weights,
):
    tile_rows, tile_cols, channels = pair_state.shape
    hidden = output_weights.shape[1]
    row_count = lax.axis_size("row")
    col_count = lax.axis_size("col")
    per_device = hidden // (row_count * col_count)
    current = pair_state.astype(jnp.float32)
    mask_float = pair_mask.astype(jnp.float32)[None]
    for layer_index in range(2):
        pair_ln = normalize(current, input_gain[layer_index], input_bias[layer_index], -1).astype(
            jnp.bfloat16
        )
        left_panel = gated_panel(pair_ln, proj_weights[layer_index], 0, hidden, mask_float)
        right_panel = gated_panel(
            pair_ln, proj_weights[layer_index], 2 * hidden, hidden, mask_float
        )
        gate_value = jax.nn.sigmoid(
            jnp.einsum(
                "ijd,de->ije",
                pair_ln,
                gate_weights[layer_index],
                preferred_element_type=jnp.float32,
            )
        )
        scale_out = output_gain[layer_index]
        shift_out = output_bias[layer_index]
        weight_out = output_weights[layer_index]
        left_recv, right_recv = (
            lax.all_to_all(left_panel, ("row", "col"), split_axis=0, concat_axis=1, tiled=True),
            lax.all_to_all(right_panel, ("row", "col"), split_axis=0, concat_axis=1, tiled=True),
        )
        left_chan = (
            left_recv.reshape(per_device, row_count, col_count, tile_rows, tile_cols)
            .transpose(0, 1, 3, 2, 4)
            .reshape(per_device, row_count * tile_rows, col_count * tile_cols)
        )
        right_chan = (
            right_recv.reshape(per_device, row_count, col_count, tile_rows, tile_cols)
            .transpose(0, 1, 3, 2, 4)
            .reshape(per_device, row_count * tile_rows, col_count * tile_cols)
        )
        product = contract(left_chan, right_chan, layer_index)
        arranged = (
            product.reshape(per_device, row_count, tile_rows, col_count, tile_cols)
            .transpose(0, 1, 3, 2, 4)
            .reshape(per_device, row_count * col_count * tile_rows, tile_cols)
        )
        returned = lax.all_to_all(arranged, ("row", "col"), split_axis=1, concat_axis=0, tiled=True)
        normed = normalize(
            returned.astype(jnp.float32), scale_out[:, None, None], shift_out[:, None, None], 0
        ).astype(jnp.bfloat16)
        update = jnp.einsum("cij,cd->ijd", normed, weight_out, preferred_element_type=jnp.float32)
        current = current + gate_value * update
    return current.astype(jnp.bfloat16)


MESH = pl.DeviceIdType.MESH
F32 = jnp.float32
BF16 = jnp.bfloat16


def sigmoid(values):
    return 0.5 * jnp.tanh(0.5 * values) + 0.5


def lane_groups(shape, width):
    return lax.broadcasted_iota(jnp.int32, shape, len(shape) - 1) // width


def swap_groups(blocks, width):
    count = len(blocks)
    blocks = list(blocks)
    lanes = count * width
    group = lane_groups(blocks[0].shape, width)
    step = count // 2
    while step:
        low = (group // step) % 2 == 0
        for p in range(count):
            if p & step:
                continue
            first, second = blocks[p], blocks[p + step]
            shift = step * width
            blocks[p] = jnp.where(low, first, pltpu.roll(second, shift, 1))
            blocks[p + step] = jnp.where(low, pltpu.roll(first, lanes - shift, 1), second)
        step //= 2
    return blocks


def columns_of(row_vector, lanes):
    return jnp.transpose(jnp.broadcast_to(row_vector, (lanes, row_vector.shape[1])))


def contract_first(left, right):
    return lax.dot_general(left, right, (((0,), (0,)), ((), ())), preferred_element_type=F32)


def fused_kernel(
    row_count,
    col_count,
    *refs,
):
    operands, out_ref, held = refs[:9], refs[9], refs[10:19]
    load_sem = refs[19]
    loads = [
        pltpu.make_async_copy(source, target, load_sem.at[at])
        for at, (source, target) in enumerate(zip(operands, held))
    ]
    for at in (0, 1, 2, 3, 4, 5, 6, 7, 8):
        loads[at].start()
    fused_body(row_count, col_count, loads, *held, out_ref, *refs[20:])


def fused_body(
    row_count,
    col_count,
    loads,
    z_ref,
    mask_ref,
    in_gain,
    in_bias,
    proj_ref,
    gate_ref,
    out_gain,
    out_bias,
    outw_ref,
    out_ref,
    zt_ref,
    tmp_ref,
    gain_ref,
    bias_ref,
    send1,
    recv1,
    send2,
    recv2,
    send_sem,
    recv_sem,
):
    tile_rows, tile_cols, channels = z_ref.shape
    pairs = tile_rows * tile_cols
    devices = row_count * col_count
    hidden = outw_ref.shape[1]
    own = hidden // devices
    lanes = own * tile_cols
    blocks = pairs // lanes
    tokens = row_count * tile_rows
    row, col = lax.axis_index("row"), lax.axis_index("col")
    me = row * col_count + col

    half = col_count // 2
    near, inner = col // half, lax.rem(col, half)

    def place(turn, step):
        if turn < half:
            tcol = (1 - near) * half + lax.rem(2 * half - 1 - inner + turn, half)
            trow = lax.rem(2 * row_count - 1 - row + step, row_count)
        else:
            tcol = near * half + lax.rem(inner + 1 + turn - half, half)
            trow = lax.rem(row + 1 + step, row_count)
        return trow * col_count + tcol, trow, tcol

    def each(action):
        for turn in range(col_count):

            def body(step, carry, turn=turn):
                action(turn, step)
                return carry

            lax.fori_loop(0, row_count - (turn == col_count - 1), body, 0, unroll=True)

    barrier = pltpu.get_barrier_semaphore()

    def greet(turn, step):
        _, trow, tcol = place(turn, step)
        pl.semaphore_signal(barrier, inc=1, device_id=(trow, tcol), device_id_type=MESH)

    each(greet)

    def copy_panels(layer, turn, step):
        target, trow, tcol = place(turn, step)
        return pltpu.make_async_remote_copy(
            src_ref=send1.at[layer, target],
            dst_ref=recv1.at[layer, col, row],
            send_sem=send_sem.at[2 * layer],
            recv_sem=recv_sem.at[2 * layer],
            device_id=(trow, tcol),
            device_id_type=MESH,
        )

    def copy_product(layer, turn, step):
        target, trow, tcol = place(turn, step)
        return pltpu.make_async_remote_copy(
            src_ref=send2.at[layer, tcol, trow],
            dst_ref=recv2.at[layer, me],
            send_sem=send_sem.at[2 * layer + 1],
            recv_sem=recv_sem.at[2 * layer + 1],
            device_id=(trow, tcol),
            device_id_type=MESH,
        )

    def start_all(make, layer):
        each(lambda turn, step: make(layer, turn, step).start())

    def wait_panels(sem, layer):
        slots = send1.at[layer, pl.ds(0, devices - 1)]
        pltpu.make_async_copy(slots, slots, sem.at[2 * layer]).wait()

    def wait_products(sem, layer):
        slots = recv2.at[layer, pl.ds(0, devices - 1)]
        pltpu.make_async_copy(slots, slots, sem.at[2 * layer + 1]).wait()

    loads[0].wait()
    zt_ref[...] = jnp.transpose(z_ref[...].astype(F32).reshape(pairs, channels))
    for at in range(1, len(loads)):
        loads[at].wait()
    spread = (
        lax.broadcasted_iota(jnp.int32, (tile_cols, pairs), 1) % tile_cols
        == lax.broadcasted_iota(jnp.int32, (tile_cols, pairs), 0)
    ).astype(F32)
    mine = (
        lax.broadcasted_iota(jnp.int32, (tile_rows, pairs), 1) // tile_cols
        == lax.broadcasted_iota(jnp.int32, (tile_rows, pairs), 0)
    ).astype(F32)
    mask_flat = jnp.sum(
        jnp.dot(mask_ref[...].astype(F32), spread, preferred_element_type=F32) * mine,
        axis=0,
        keepdims=True,
    )

    for layer in range(2):
        current = zt_ref[...]
        centred = current - jnp.mean(current, axis=0, keepdims=True)
        scale = lax.rsqrt(jnp.mean(centred * centred, axis=0, keepdims=True) + epsilon)
        gain = columns_of(in_gain[layer : layer + 1, :], lanes)
        bias = columns_of(in_bias[layer : layer + 1, :], lanes)
        gain = jnp.concatenate([gain] * blocks, axis=1)
        bias = jnp.concatenate([bias] * blocks, axis=1)
        normed = (centred * scale * gain + bias).astype(BF16)
        projected = contract_first(proj_ref[layer], normed)
        for side in range(2):
            first = 2 * side * hidden
            panel = (
                sigmoid(projected[first : first + hidden])
                * projected[first + hidden : first + 2 * hidden]
                * mask_flat
            )
            for block in range(blocks):
                parts = [
                    panel[k * devices : (k + 1) * devices, block * lanes : (block + 1) * lanes]
                    for k in range(own)
                ]
                for q, part in enumerate(swap_groups(parts, tile_cols)):
                    line = block * own + q
                    tmp_ref[side, line * devices : (line + 1) * devices, :] = part
            for target in range(devices):
                send1[layer, target, side] = tmp_ref[
                    side, pl.ds(target, tile_rows, stride=devices), :
                ].astype(BF16)
        if layer == 0:
            pl.semaphore_wait(barrier, devices - 1)
        start_all(copy_panels, layer)
        recv1[layer, col, row] = send1[layer, me]
        gate_value = sigmoid(contract_first(gate_ref[layer], normed))
        group = lane_groups((devices, lanes), tile_cols)
        for source, kept in ((out_gain, gain_ref), (out_bias, bias_ref)):
            wide = columns_of(source[layer : layer + 1, :], lanes)
            packed = wide[0:devices]
            for k in range(1, own):
                packed = jnp.where(group == k, wide[k * devices : (k + 1) * devices], packed)
            kept[...] = packed
        wait_panels(recv_sem, layer)

        left = jnp.concatenate(
            [recv1[layer, c, :, 0].reshape(tokens, lanes) for c in range(col_count)], axis=1
        )
        right = jnp.concatenate(
            [recv1[layer, c, :, 1].reshape(tokens, lanes) for c in range(col_count)], axis=1
        )
        if layer == 0:
            wide_group = lane_groups((1, col_count * lanes), tile_cols) % own
            masks = [(wide_group == k).astype(F32).astype(BF16) for k in range(own)]
            for c in range(col_count):
                rows = right[c * tile_cols : (c + 1) * tile_cols]
                stacked = jnp.concatenate([rows * masks[k] for k in range(own)], axis=0)
                product = lax.dot_general(
                    left, stacked, (((1,), (1,)), ((), ())), preferred_element_type=F32
                )
                send2[layer, c] = product.astype(BF16).reshape(row_count, tile_rows, lanes)
        else:
            product = contract_first(left, right)
            group = lane_groups((tile_cols, lanes), tile_cols)
            for c in range(col_count):
                pieces = []
                for d in range(col_count):
                    at = d * lanes
                    piece = product[at : at + tile_cols, c * lanes : (c + 1) * lanes]
                    for k in range(1, own):
                        low = at + k * tile_cols
                        piece = jnp.where(
                            group == k,
                            product[low : low + tile_cols, c * lanes : (c + 1) * lanes],
                            piece,
                        )
                    pieces.append(piece.astype(BF16))
                send2[layer, c] = jnp.concatenate(pieces, axis=0).reshape(
                    row_count, tile_rows, lanes
                )
        start_all(copy_product, layer)
        recv2[layer, me] = send2[layer, col, row]
        wait_products(recv_sem, layer)

        returned = recv2[layer].astype(F32)

        def over_channels(values):
            total = jnp.sum(values, axis=0)
            shift = lanes // 2
            while shift >= tile_cols:
                total = total + pltpu.roll(total, shift, 1)
                shift //= 2
            return total * (1.0 / hidden)

        centred = returned - over_channels(returned)[None]
        scale = lax.rsqrt(over_channels(centred * centred) + epsilon)
        for d in range(devices):
            tmp_ref[0, d * tile_rows : (d + 1) * tile_rows, :] = (
                centred[d] * scale * gain_ref[d : d + 1, :] + bias_ref[d : d + 1, :]
            )
        wide_blocks = []
        for block in range(blocks):
            parts = [
                tmp_ref[0, pl.ds(block * own + q, devices, stride=tile_rows), :] for q in range(own)
            ]
            wide_blocks.append(
                jnp.concatenate(swap_groups(parts, tile_cols), axis=0).astype(BF16)
            )
        update = contract_first(outw_ref[layer], jnp.concatenate(wide_blocks, axis=1))
        zt_ref[...] = zt_ref[...] + gate_value * update

    out_ref[...] = (
        jnp.transpose(zt_ref[...]).reshape(tile_rows, tile_cols, channels).astype(BF16)
    )
    for layer in range(2):
        wait_panels(send_sem, layer)
        wait_products(send_sem, layer)


def fused(row_count, col_count, *args):
    tile_rows, tile_cols, channels = args[0].shape
    devices = row_count * col_count
    hidden = args[-1].shape[1]
    lanes = hidden // devices * tile_cols
    pairs = tile_rows * tile_cols
    vmem = pl.BlockSpec(memory_space=pltpu.VMEM)
    return pl.pallas_call(
        functools.partial(fused_kernel, row_count, col_count),
        out_shape=jax.ShapeDtypeStruct(args[0].shape, BF16),
        in_specs=[pl.BlockSpec(memory_space=pl.ANY)] * len(args),
        out_specs=vmem,
        scratch_shapes=[pltpu.VMEM(arg.shape, arg.dtype) for arg in args]
        + [
            pltpu.SemaphoreType.DMA((len(args),)),
            pltpu.VMEM((channels, pairs), F32),
            pltpu.VMEM((2, tile_rows * devices, lanes), F32),
            pltpu.VMEM((devices, lanes), F32),
            pltpu.VMEM((devices, lanes), F32),
            pltpu.VMEM((2, devices, 2, tile_rows, lanes), BF16),
            pltpu.VMEM((2, col_count, row_count, 2, tile_rows, lanes), BF16),
            pltpu.VMEM((2, col_count, row_count, tile_rows, lanes), BF16),
            pltpu.VMEM((2, devices, tile_rows, lanes), BF16),
            pltpu.SemaphoreType.DMA((4,)),
            pltpu.SemaphoreType.DMA((4,)),
        ],
        compiler_params=pltpu.CompilerParams(collective_id=0, has_side_effects=True),
    )(*args)


def solution(mesh):
    row_count, col_count = mesh.shape["row"], mesh.shape["col"]
    devices = row_count * col_count

    def step(*args):
        tile_rows, tile_cols, channels = args[0].shape
        hidden = args[-1].shape[1]
        own = hidden // devices
        fits = (
            hidden % devices == 0
            and own * tile_cols == 128
            and tile_rows % 16 == 0
            and tile_rows % own == 0
            and own & (own - 1) == 0
            and col_count % 2 == 0
            and row_count * tile_rows == col_count * tile_cols
        )
        return fused(row_count, col_count, *args) if fits else on_device(*args)

    return jax.shard_map(
        step,
        mesh=mesh,
        in_specs=(P("row", "col", None), P("row", "col"), P(), P(), P(), P(), P(), P(), P()),
        out_specs=P("row", "col", None),
        check_vma=False,
    )
```

profile of v0, /device:TPU:0, one launch (start us, length us, event | category | flops | bytes accessed | tf_op | source)
XLA Modules:
  0.0 38.6 jit_solution(9817839605650998213)
XLA Ops:
  0.0 37.0 %shard_map.91 = bf16[16,32,128]{2,1,0:T(8,128)(2,1)} custom-call(bf16[16,32,128]{2,1,0:T(8,128)(2,1)} %refs_0_.1, s32[16,32]{1,0:T(8,128)} %refs_1_.1, f32[2,128]{1,0:T(2,128)} %refs_2_.1, f32[2,128]{1,0:T(2,128)} %refs_3_.1, bf16[2,128,512]{2,1,0:T(8,128)(2,1)} %refs_4_.1, bf16[2,128,128]{2,1,0:T(8,128)(2,1)} %refs_5_.1, f32[2,128]{1,0:T(2,128)} %refs_6_.1, ...), custom_call_target="tpu_custom_call" | custom-call | tf_op jit(solution)/shard_map/pallas_call | solution.py:406
  37.0 1.6 %copy.11 = bf16[16,32,128]{2,1,0:T(8,128)(2,1)} copy(bf16[16,32,128]{2,1,0:T(8,128)(2,1)} %shard_map.91) | data formatting | bytes 262144
where the time goes:
time: 38.8 us; the launch traced here: 38.6 us
  Pallas kernels  37 us (95%)
  local copies, waits for them, and re-layouts  1.57 us (4%)
    pallas_call x1, Pallas kernels, fused(): pl.pallas_call(functools.partial(fused_kernel, row_count, col_count), out...  37 us
    unnamed x1, local copies, waits for them, and re-layouts  1.57 us

commit v1 on v0

v1 whole, which is shorter than its diff:
```python
import functools

import jax
import jax.numpy as jnp
from jax import lax
from jax.experimental import pallas as pl
from jax.experimental.pallas import tpu as pltpu
from jax.sharding import PartitionSpec as P

epsilon = 1e-05


def normalize(values, weight_scale, weight_shift, reduce_axis):
    average = jnp.mean(values, axis=reduce_axis, keepdims=True)
    centred = values - average
    spread = jnp.mean(centred * centred, axis=reduce_axis, keepdims=True)
    return centred * lax.rsqrt(spread + epsilon) * weight_scale + weight_shift


def contract(left_panel, right_panel, layer_index):
    if layer_index == 0:
        product = jnp.einsum(
            "cik,cjk->cij", left_panel, right_panel, preferred_element_type=jnp.float32
        )
    else:
        product = jnp.einsum(
            "cki,ckj->cij", left_panel, right_panel, preferred_element_type=jnp.float32
        )
    return product.astype(jnp.bfloat16)


def gated_panel(pair_ln, weights, first, hidden, mask_float):
    projected = jnp.einsum(
        "ijd,de->eij",
        pair_ln,
        weights[:, first : first + 2 * hidden],
        preferred_element_type=jnp.float32,
    )
    return (jax.nn.sigmoid(projected[:hidden]) * projected[hidden:] * mask_float).astype(
        jnp.bfloat16
    )


def on_device(
    pair_state,
    pair_mask,
    input_gain,
    input_bias,
    proj_weights,
    gate_weights,
    output_gain,
    output_bias,
    output_weights,
):
    tile_rows, tile_cols, channels = pair_state.shape
    hidden = output_weights.shape[1]
    row_count = lax.axis_size("row")
    col_count = lax.axis_size("col")
    per_device = hidden // (row_count * col_count)
    current = pair_state.astype(jnp.float32)
    mask_float = pair_mask.astype(jnp.float32)[None]
    for layer_index in range(2):
        pair_ln = normalize(current, input_gain[layer_index], input_bias[layer_index], -1).astype(
            jnp.bfloat16
        )
        left_panel = gated_panel(pair_ln, proj_weights[layer_index], 0, hidden, mask_float)
        right_panel = gated_panel(
            pair_ln, proj_weights[layer_index], 2 * hidden, hidden, mask_float
        )
        gate_value = jax.nn.sigmoid(
            jnp.einsum(
                "ijd,de->ije",
                pair_ln,
                gate_weights[layer_index],
                preferred_element_type=jnp.float32,
            )
        )
        scale_out = output_gain[layer_index]
        shift_out = output_bias[layer_index]
        weight_out = output_weights[layer_index]
        left_recv, right_recv = (
            lax.all_to_all(left_panel, ("row", "col"), split_axis=0, concat_axis=1, tiled=True),
            lax.all_to_all(right_panel, ("row", "col"), split_axis=0, concat_axis=1, tiled=True),
        )
        left_chan = (
            left_recv.reshape(per_device, row_count, col_count, tile_rows, tile_cols)
            .transpose(0, 1, 3, 2, 4)
            .reshape(per_device, row_count * tile_rows, col_count * tile_cols)
        )
        right_chan = (
            right_recv.reshape(per_device, row_count, col_count, tile_rows, tile_cols)
            .transpose(0, 1, 3, 2, 4)
            .reshape(per_device, row_count * tile_rows, col_count * tile_cols)
        )
        product = contract(left_chan, right_chan, layer_index)
        arranged = (
            product.reshape(per_device, row_count, tile_rows, col_count, tile_cols)
            .transpose(0, 1, 3, 2, 4)
            .reshape(per_device, row_count * col_count * tile_rows, tile_cols)
        )
        returned = lax.all_to_all(arranged, ("row", "col"), split_axis=1, concat_axis=0, tiled=True)
        normed = normalize(
            returned.astype(jnp.float32), scale_out[:, None, None], shift_out[:, None, None], 0
        ).astype(jnp.bfloat16)
        update = jnp.einsum("cij,cd->ijd", normed, weight_out, preferred_element_type=jnp.float32)
        current = current + gate_value * update
    return current.astype(jnp.bfloat16)


MESH = pl.DeviceIdType.MESH
F32 = jnp.float32
BF16 = jnp.bfloat16
CHUNKS = 2


def sigmoid(values):
    return 0.5 * jnp.tanh(0.5 * values) + 0.5


def lane_groups(shape, width):
    return lax.broadcasted_iota(jnp.int32, shape, len(shape) - 1) // width


def swap_groups(blocks, width):
    count = len(blocks)
    blocks = list(blocks)
    lanes = count * width
    group = lane_groups(blocks[0].shape, width)
    step = count // 2
    while step:
        low = (group // step) % 2 == 0
        for p in range(count):
            if p & step:
                continue
            first, second = blocks[p], blocks[p + step]
            shift = step * width
            blocks[p] = jnp.where(low, first, pltpu.roll(second, shift, 1))
            blocks[p + step] = jnp.where(low, pltpu.roll(first, lanes - shift, 1), second)
        step //= 2
    return blocks


def columns_of(row_vector, lanes):
    return jnp.transpose(jnp.broadcast_to(row_vector, (lanes, row_vector.shape[1])))


def contract_first(left, right):
    return lax.dot_general(left, right, (((0,), (0,)), ((), ())), preferred_element_type=F32)


def fused_kernel(row_count, col_count, *refs):
    operands, out_ref, held = refs[:9], refs[9], refs[10:19]
    load_sem = refs[19]
    loads = [
        pltpu.make_async_copy(source, target, load_sem.at[at])
        for at, (source, target) in enumerate(zip(operands, held))
    ]
    for at in (0, 4, 2, 3, 1, 5, 6, 7, 8):
        loads[at].start()
    fused_body(row_count, col_count, loads, *held, out_ref, *refs[20:])


def fused_body(
    row_count,
    col_count,
    loads,
    z_ref,
    mask_ref,
    in_gain,
    in_bias,
    proj_ref,
    gate_ref,
    out_gain,
    out_bias,
    outw_ref,
    out_ref,
    zt_ref,
    tmp_ref,
    gated_ref,
    in_gain_ref,
    in_bias_ref,
    gain_ref,
    bias_ref,
    send1,
    recv_k,
    recv_a,
    recv_b,
    send_sum,
    recv_sum,
    send_own,
    recv_own,
    send_sem,
    recv_sem,
):
    tile_rows, tile_cols, channels = z_ref.shape
    devices = row_count * col_count
    hidden = outw_ref.shape[1]
    half = col_count // 2
    width = tile_cols // CHUNKS
    pairs = tile_rows * width
    owners = row_count * half
    own = hidden // owners
    lanes = own * width
    blocks = pairs // lanes
    tokens = row_count * tile_rows
    row, col = lax.axis_index("row"), lax.axis_index("col")
    near, inner = col // half, lax.rem(col, half)
    me = row * half + inner

    def place(turn, step):
        if turn < half:
            tcol = (1 - near) * half + lax.rem(2 * half - 1 - inner + turn, half)
            trow = lax.rem(2 * row_count - 1 - row + step, row_count)
        else:
            tcol = near * half + lax.rem(inner + 1 + turn - half, half)
            trow = lax.rem(row + 1 + step, row_count)
        return trow, tcol

    def each(action, first=0):
        for turn in range(first, col_count):

            def body(step, carry, turn=turn):
                action(*place(turn, step))
                return carry

            lax.fori_loop(0, row_count - (turn == col_count - 1), body, 0, unroll=True)

    barrier = pltpu.get_barrier_semaphore()

    def greet(trow, tcol):
        pl.semaphore_signal(barrier, inc=1, device_id=(trow, tcol), device_id_type=MESH)

    each(greet)

    def send(source, target, at, trow, tcol):
        pltpu.make_async_remote_copy(
            src_ref=source,
            dst_ref=target,
            send_sem=send_sem.at[at],
            recv_sem=recv_sem.at[at],
            device_id=(trow, tcol),
            device_id_type=MESH,
        ).start()

    def owner(trow, tcol):
        return trow * half + lax.rem(tcol, half)

    slot = inner * row_count + row

    def start_k(chunk):
        each(
            lambda trow, tcol: send(
                send1.at[0, chunk, owner(trow, tcol)], recv_k.at[chunk, slot], chunk, trow, tcol
            ),
            half,
        )
        recv_k[chunk, slot] = send1[0, chunk, me]

    def wait_k(sem, chunk):
        slots = recv_k.at[chunk, pl.ds(0, owners - 1)]
        pltpu.make_async_copy(slots, slots, sem.at[chunk]).wait()

    def start_sum(chunk):
        each(
            lambda trow, tcol: send(
                send_sum.at[chunk, tcol, trow],
                recv_sum.at[chunk, near * owners + me],
                CHUNKS + chunk,
                trow,
                tcol,
            )
        )
        recv_sum[chunk, near * owners + me] = send_sum[chunk, col, row]

    def wait_sum(sem, chunk):
        slots = recv_sum.at[chunk, pl.ds(0, devices - 1)]
        pltpu.make_async_copy(slots, slots, sem.at[CHUNKS + chunk]).wait()

    def start_ab(chunk):
        each(
            lambda trow, tcol: send(
                send1.at[1, chunk, owner(trow, tcol), 0],
                recv_a.at[chunk, col * row_count + row],
                2 * CHUNKS + chunk,
                trow,
                tcol,
            )
        )
        each(
            lambda trow, tcol: send(
                send1.at[1, chunk, owner(trow, tcol), 1],
                recv_b.at[chunk, slot],
                3 * CHUNKS + chunk,
                trow,
                tcol,
            ),
            half,
        )
        recv_a[chunk, col * row_count + row] = send1[1, chunk, me, 0]
        recv_b[chunk, slot] = send1[1, chunk, me, 1]

    def wait_ab(sem, chunk):
        slots = recv_a.at[chunk, pl.ds(0, devices - 1)]
        pltpu.make_async_copy(slots, slots, sem.at[2 * CHUNKS + chunk]).wait()
        slots = recv_b.at[chunk, pl.ds(0, owners - 1)]
        pltpu.make_async_copy(slots, slots, sem.at[3 * CHUNKS + chunk]).wait()

    def start_own(chunk):
        each(
            lambda trow, tcol: send(
                send_own.at[chunk, lax.rem(tcol, half), trow],
                recv_own.at[chunk, me],
                4 * CHUNKS + chunk,
                trow,
                tcol,
            ),
            half,
        )
        recv_own[chunk, me] = send_own[chunk, inner, row]

    def wait_own(sem, chunk):
        slots = recv_own.at[chunk, pl.ds(0, owners - 1)]
        pltpu.make_async_copy(slots, slots, sem.at[4 * CHUNKS + chunk]).wait()

    def spread_inputs(layer):
        in_gain_ref[layer] = columns_of(in_gain[layer : layer + 1, :], lanes)
        in_bias_ref[layer] = columns_of(in_bias[layer : layer + 1, :], lanes)

    def spread_outputs(layer):
        group = lane_groups((owners, lanes), width)
        for source, kept in ((out_gain, gain_ref), (out_bias, bias_ref)):
            wide = columns_of(source[layer : layer + 1, :], lanes)
            packed = wide[0:owners]
            for k in range(1, own):
                packed = jnp.where(group == k, wide[k * owners : (k + 1) * owners], packed)
            kept[layer] = packed

    def front(layer, chunk, current, mask_flat):
        centred = current - jnp.mean(current, axis=0, keepdims=True)
        scale = lax.rsqrt(jnp.mean(centred * centred, axis=0, keepdims=True) + epsilon)
        gain = jnp.concatenate([in_gain_ref[layer]] * blocks, axis=1)
        bias = jnp.concatenate([in_bias_ref[layer]] * blocks, axis=1)
        normed = (centred * scale * gain + bias).astype(BF16)
        projected = contract_first(proj_ref[layer], normed)
        for side in range(2):
            first = 2 * side * hidden
            panel = (
                sigmoid(projected[first : first + hidden])
                * projected[first + hidden : first + 2 * hidden]
                * mask_flat
            )
            for block in range(blocks):
                parts = [
                    panel[k * owners : (k + 1) * owners, block * lanes : (block + 1) * lanes]
                    for k in range(own)
                ]
                for q, part in enumerate(swap_groups(parts, width)):
                    line = block * own + q
                    tmp_ref[side, line * owners : (line + 1) * owners, :] = part
            for target in range(owners):
                send1[layer, chunk, target, side] = tmp_ref[
                    side, pl.ds(target, tile_rows, stride=owners), :
                ].astype(BF16)
        return normed

    def gate(layer, chunk, normed):
        gated_ref[chunk] = sigmoid(contract_first(gate_ref[layer], normed))

    def over_channels(values):
        total = jnp.sum(values, axis=0)
        shift = lanes // 2
        while shift >= width:
            total = total + pltpu.roll(total, shift, 1)
            shift //= 2
        return total * (1.0 / hidden)

    def back(layer, chunk, returned):
        centred = returned - over_channels(returned)[None]
        scale = lax.rsqrt(over_channels(centred * centred) + epsilon)
        for d in range(owners):
            tmp_ref[0, d * tile_rows : (d + 1) * tile_rows, :] = (
                centred[d] * scale * gain_ref[layer, d : d + 1, :] + bias_ref[layer, d : d + 1, :]
            )
        wide_blocks = []
        for block in range(blocks):
            parts = [
                tmp_ref[0, pl.ds(block * own + q, owners, stride=tile_rows), :] for q in range(own)
            ]
            wide_blocks.append(jnp.concatenate(swap_groups(parts, width), axis=0).astype(BF16))
        update = contract_first(outw_ref[layer], jnp.concatenate(wide_blocks, axis=1))
        return zt_ref[chunk] + gated_ref[chunk] * update

    for at in (2, 3):
        loads[at].wait()
    spread_inputs(0)
    loads[1].wait()
    mask_float = mask_ref[...].astype(F32)
    across = lax.broadcasted_iota(jnp.int32, (tile_cols, pairs), 1) % width
    mine = (
        lax.broadcasted_iota(jnp.int32, (tile_rows, pairs), 1) // width
        == lax.broadcasted_iota(jnp.int32, (tile_rows, pairs), 0)
    ).astype(F32)
    mask_flat = []
    for chunk in range(CHUNKS):
        spread = (
            across + chunk * width == lax.broadcasted_iota(jnp.int32, (tile_cols, pairs), 0)
        ).astype(F32)
        mask_flat.append(
            jnp.sum(
                jnp.dot(mask_float, spread, preferred_element_type=F32) * mine,
                axis=0,
                keepdims=True,
            )
        )
    loads[0].wait()
    loads[4].wait()
    normed = [None] * CHUNKS
    for chunk in range(CHUNKS):
        zt_ref[chunk] = jnp.transpose(
            z_ref[:, chunk * width : (chunk + 1) * width, :].astype(F32).reshape(pairs, channels)
        )
        normed[chunk] = front(0, chunk, zt_ref[chunk], mask_flat[chunk])
        if chunk == 0:
            pl.semaphore_wait(barrier, devices - 1)
        start_k(chunk)
    for at in (5, 6, 7, 8):
        loads[at].wait()
    for chunk in range(CHUNKS):
        gate(0, chunk, normed[chunk])
    spread_inputs(1)
    for layer in range(2):
        spread_outputs(layer)
    for chunk in range(CHUNKS):
        wait_k(recv_sem, chunk)

    def panel(ref, chunk, plane, *side):
        return ref[
            (chunk, slice(plane * row_count, (plane + 1) * row_count)) + side
        ].reshape(tokens, lanes)

    spans = [(chunk, plane) for chunk in range(CHUNKS) for plane in range(half)]
    left = jnp.concatenate([panel(recv_k, c, p, 0) for c, p in spans], axis=1)
    right = jnp.concatenate([panel(recv_k, c, p, 1) for c, p in spans], axis=1)
    lane_group = lane_groups((1, len(spans) * lanes), width) % own
    masks = [(lane_group == k).astype(F32).astype(BF16) for k in range(own)]
    for chunk in range(CHUNKS):
        for c in range(col_count):
            at = (c * CHUNKS + chunk) * width
            rows = right[at : at + width]
            stacked = jnp.concatenate([rows * masks[k] for k in range(own)], axis=0)
            product = lax.dot_general(
                left, stacked, (((1,), (1,)), ((), ())), preferred_element_type=F32
            )
            send_sum[chunk, c] = product.astype(BF16).reshape(row_count, tile_rows, lanes)
        start_sum(chunk)

    for chunk in range(CHUNKS):
        wait_sum(recv_sem, chunk)
        returned = recv_sum[chunk, 0:owners].astype(F32) + recv_sum[
            chunk, owners : 2 * owners
        ].astype(F32)
        zt_ref[chunk] = back(0, chunk, returned)
        normed[chunk] = front(1, chunk, zt_ref[chunk], mask_flat[chunk])
        start_ab(chunk)
    for chunk in range(CHUNKS):
        gate(1, chunk, normed[chunk])
    for chunk in range(CHUNKS):
        wait_ab(recv_sem, chunk)

    left = jnp.concatenate(
        [panel(recv_a, chunk, c) for c in range(col_count) for chunk in range(CHUNKS)], axis=1
    )
    group = lane_groups((width, lanes), width)
    for chunk in range(CHUNKS):
        right = jnp.concatenate([panel(recv_b, chunk, p) for p in range(half)], axis=1)
        product = contract_first(left, right)
        for p in range(half):
            for r in range(row_count):
                at = r * lanes
                piece = product[at : at + width, p * lanes : (p + 1) * lanes]
                for k in range(1, own):
                    low = at + k * width
                    piece = jnp.where(
                        group == k,
                        product[low : low + width, p * lanes : (p + 1) * lanes],
                        piece,
                    )
                send_own[chunk, p, r] = piece.astype(BF16)
        start_own(chunk)

    for chunk in range(CHUNKS):
        wait_own(recv_sem, chunk)
        final = back(1, chunk, recv_own[chunk].astype(F32))
        out_ref[:, chunk * width : (chunk + 1) * width, :] = (
            jnp.transpose(final).reshape(tile_rows, width, channels).astype(BF16)
        )
    for chunk in range(CHUNKS):
        wait_k(send_sem, chunk)
        wait_sum(send_sem, chunk)
        wait_ab(send_sem, chunk)
        wait_own(send_sem, chunk)


def fused(row_count, col_count, *args):
    tile_rows, tile_cols, channels = args[0].shape
    devices = row_count * col_count
    hidden = args[-1].shape[1]
    half = col_count // 2
    owners = row_count * half
    width = tile_cols // CHUNKS
    lanes = hidden // owners * width
    pairs = tile_rows * width
    vmem = pl.BlockSpec(memory_space=pltpu.VMEM)
    return pl.pallas_call(
        functools.partial(fused_kernel, row_count, col_count),
        out_shape=jax.ShapeDtypeStruct(args[0].shape, BF16),
        in_specs=[pl.BlockSpec(memory_space=pl.ANY)] * len(args),
        out_specs=vmem,
        scratch_shapes=[pltpu.VMEM(arg.shape, arg.dtype) for arg in args]
        + [
            pltpu.SemaphoreType.DMA((len(args),)),
            pltpu.VMEM((CHUNKS, channels, pairs), F32),
            pltpu.VMEM((2, tile_rows * owners, lanes), F32),
            pltpu.VMEM((CHUNKS, channels, pairs), F32),
            pltpu.VMEM((2, channels, lanes), F32),
            pltpu.VMEM((2, channels, lanes), F32),
            pltpu.VMEM((2, owners, lanes), F32),
            pltpu.VMEM((2, owners, lanes), F32),
            pltpu.VMEM((2, CHUNKS, owners, 2, tile_rows, lanes), BF16),
            pltpu.VMEM((CHUNKS, owners, 2, tile_rows, lanes), BF16),
            pltpu.VMEM((CHUNKS, devices, tile_rows, lanes), BF16),
            pltpu.VMEM((CHUNKS, owners, tile_rows, lanes), BF16),
            pltpu.VMEM((CHUNKS, col_count, row_count, tile_rows, lanes), BF16),
            pltpu.VMEM((CHUNKS, devices, tile_rows, lanes), BF16),
            pltpu.VMEM((CHUNKS, half, row_count, tile_rows, lanes), BF16),
            pltpu.VMEM((CHUNKS, owners, tile_rows, lanes), BF16),
            pltpu.SemaphoreType.DMA((5 * CHUNKS,)),
            pltpu.SemaphoreType.DMA((5 * CHUNKS,)),
        ],
        compiler_params=pltpu.CompilerParams(collective_id=0, has_side_effects=True),
    )(*args)


def solution(mesh):
    row_count, col_count = mesh.shape["row"], mesh.shape["col"]
    devices = row_count * col_count

    def step(*args):
        tile_rows, tile_cols, channels = args[0].shape
        hidden = args[-1].shape[1]
        owners = devices // 2
        own = hidden // owners
        width = tile_cols // CHUNKS
        fits = (
            hidden % devices == 0
            and col_count % 2 == 0
            and tile_cols % CHUNKS == 0
            and own * width == 128
            and tile_rows == width
            and tile_rows % 16 == 0
            and tile_rows % own == 0
            and own & (own - 1) == 0
            and row_count * tile_rows == col_count * tile_cols
        )
        return fused(row_count, col_count, *args) if fits else on_device(*args)

    return jax.shard_map(
        step,
        mesh=mesh,
        in_specs=(P("row", "col", None), P("row", "col"), P(), P(), P(), P(), P(), P(), P()),
        out_specs=P("row", "col", None),
        check_vma=False,
    )
```

time: 38.8 us -> 37.9 us (0.977)
  Pallas kernels: 37 us -> 36.2 us
    pallas_call x1, Pallas kernels: 37 us -> 36.2 us  [fused(): pl.pallas_call(functools.partial(fused_kernel, row_count, col_count), out...]
where the time goes in v1:
time: 37.9 us; the launch traced here: 37.8 us
  Pallas kernels  36.2 us (96%)
  local copies, waits for them, and re-layouts  1.57 us (4%)
    pallas_call x1, Pallas kernels, fused(): pl.pallas_call(functools.partial(fused_kernel, row_count, col_count), out...  36.2 us
    unnamed x1, local copies, waits for them, and re-layouts  1.57 us

profile of v1, /device:TPU:0, one launch (start us, length us, event | category | flops | bytes accessed | tf_op | source)
XLA Modules:
  0.0 37.8 jit_solution(2670535764972593615)
XLA Ops:
  0.0 36.2 %shard_map.91 = bf16[16,32,128]{2,1,0:T(8,128)(2,1)} custom-call(bf16[16,32,128]{2,1,0:T(8,128)(2,1)} %refs_0_.1, s32[16,32]{1,0:T(8,128)} %refs_1_.1, f32[2,128]{1,0:T(2,128)} %refs_2_.1, f32[2,128]{1,0:T(2,128)} %refs_3_.1, bf16[2,128,512]{2,1,0:T(8,128)(2,1)} %refs_4_.1, bf16[2,128,128]{2,1,0:T(8,128)(2,1)} %refs_5_.1, f32[2,128]{1,0:T(2,128)} %refs_6_.1, ...), custom_call_target="tpu_custom_call" | custom-call | tf_op jit(solution)/shard_map/pallas_call | solution.py:514
  36.2 1.6 %copy.11 = bf16[16,32,128]{2,1,0:T(8,128)(2,1)} copy(bf16[16,32,128]{2,1,0:T(8,128)(2,1)} %shard_map.91) | data formatting | bytes 262144

commit v2 on v1

--- a/solution.py
+++ b/solution.py
@@ -181,10 +181,11 @@
     in_bias_ref,
     gain_ref,
     bias_ref,
-    send1,
+    send_k,
     recv_k,
+    send_ab,
     recv_a,
-    recv_b,
+    recv_ab,
     send_sum,
     recv_sum,
     send_own,
@@ -207,30 +208,36 @@
     near, inner = col // half, lax.rem(col, half)
     me = row * half + inner
 
-    def place(turn, step):
-        if turn < half:
-            tcol = (1 - near) * half + lax.rem(2 * half - 1 - inner + turn, half)
-            trow = lax.rem(2 * row_count - 1 - row + step, row_count)
-        else:
-            tcol = near * half + lax.rem(inner + 1 + turn - half, half)
-            trow = lax.rem(row + 1 + step, row_count)
-        return trow, tcol
-
-    def each(action, first=0):
-        for turn in range(first, col_count):
-
-            def body(step, carry, turn=turn):
-                action(*place(turn, step))
-                return carry
-
-            lax.fori_loop(0, row_count - (turn == col_count - 1), body, 0, unroll=True)
+    def flips(index, count):
+        bits = count.bit_length() - 1
+        moves = [(1 << b) * (1 - 2 * lax.rem(index // (1 << b), 2)) for b in range(bits)]
+
+        def flipped(pattern):
+            total = index
+            for b in range(bits):
+                if pattern >> b & 1:
+                    total = total + moves[b]
+            return total
+
+        return [flipped(pattern) for pattern in range(count)]
+
+    rows, cols = flips(row, row_count), flips(col, col_count)
+    row_order = sorted(range(row_count), key=lambda p: (-p.bit_count(), -p))
+    across = list(range(half, col_count))
+    within = list(range(half - 1, -1, -1))
+
+    def each(action, turns):
+        for turn in turns:
+            for step in row_order:
+                if turn or step:
+                    action(rows[step], cols[turn])
 
     barrier = pltpu.get_barrier_semaphore()
 
     def greet(trow, tcol):
         pl.semaphore_signal(barrier, inc=1, device_id=(trow, tcol), device_id_type=MESH)
 
-    each(greet)
+    each(greet, across + within)
 
     def send(source, target, at, trow, tcol):
         pltpu.make_async_remote_copy(
@@ -247,18 +254,16 @@
 
     slot = inner * row_count + row
 
-    def start_k(chunk):
+    def start_k():
         each(
-            lambda trow, tcol: send(
-                send1.at[0, chunk, owner(trow, tcol)], recv_k.at[chunk, slot], chunk, trow, tcol
-            ),
-            half,
-        )
-        recv_k[chunk, slot] = send1[0, chunk, me]
-
-    def wait_k(sem, chunk):
-        slots = recv_k.at[chunk, pl.ds(0, owners - 1)]
-        pltpu.make_async_copy(slots, slots, sem.at[chunk]).wait()
+            lambda trow, tcol: send(send_k.at[owner(trow, tcol)], recv_k.at[slot], 0, trow, tcol),
+            within,
+        )
+        recv_k[slot] = send_k[me]
+
+    def wait_k(sem):
+        slots = recv_k.at[pl.ds(0, owners - 1)]
+        pltpu.make_async_copy(slots, slots, sem.at[0]).wait()
 
     def start_sum(chunk):
         each(
@@ -268,7 +273,8 @@
                 CHUNKS + chunk,
                 trow,
                 tcol,
-            )
+            ),
+            across + within,
         )
         recv_sum[chunk, near * owners + me] = send_sum[chunk, col, row]
 
@@ -279,30 +285,30 @@
     def start_ab(chunk):
         each(
             lambda trow, tcol: send(
-                send1.at[1, chunk, owner(trow, tcol), 0],
-                recv_a.at[chunk, col * row_count + row],
+                send_ab.at[chunk, owner(trow, tcol), 0],
+                recv_a.at[chunk, slot],
                 2 * CHUNKS + chunk,
                 trow,
                 tcol,
-            )
+            ),
+            across,
         )
         each(
             lambda trow, tcol: send(
-                send1.at[1, chunk, owner(trow, tcol), 1],
-                recv_b.at[chunk, slot],
+                send_ab.at[chunk, owner(trow, tcol)],
+                recv_ab.at[chunk, slot],
                 3 * CHUNKS + chunk,
                 trow,
                 tcol,
             ),
-            half,
-        )
-        recv_a[chunk, col * row_count + row] = send1[1, chunk, me, 0]
-        recv_b[chunk, slot] = send1[1, chunk, me, 1]
+            within,
+        )
+        recv_ab[chunk, slot] = send_ab[chunk, me]
 
     def wait_ab(sem, chunk):
-        slots = recv_a.at[chunk, pl.ds(0, devices - 1)]
+        slots = recv_a.at[chunk]
         pltpu.make_async_copy(slots, slots, sem.at[2 * CHUNKS + chunk]).wait()
-        slots = recv_b.at[chunk, pl.ds(0, owners - 1)]
+        slots = recv_ab.at[chunk, pl.ds(0, owners - 1)]
         pltpu.make_async_copy(slots, slots, sem.at[3 * CHUNKS + chunk]).wait()
 
     def start_own(chunk):
@@ -314,7 +320,7 @@
                 trow,
                 tcol,
             ),
-            half,
+            within,
         )
         recv_own[chunk, me] = send_own[chunk, inner, row]
 
@@ -335,7 +341,7 @@
                 packed = jnp.where(group == k, wide[k * owners : (k + 1) * owners], packed)
             kept[layer] = packed
 
-    def front(layer, chunk, current, mask_flat):
+    def front(layer, chunk, current, mask_flat, target_at):
         centred = current - jnp.mean(current, axis=0, keepdims=True)
         scale = lax.rsqrt(jnp.mean(centred * centred, axis=0, keepdims=True) + epsilon)
         gain = jnp.concatenate([in_gain_ref[layer]] * blocks, axis=1)
@@ -358,7 +364,7 @@
                     line = block * own + q
                     tmp_ref[side, line * owners : (line + 1) * owners, :] = part
             for target in range(owners):
-                send1[layer, chunk, target, side] = tmp_ref[
+                target_at(target)[side] = tmp_ref[
                     side, pl.ds(target, tile_rows, stride=owners), :
                 ].astype(BF16)
         return normed
@@ -395,7 +401,7 @@
     spread_inputs(0)
     loads[1].wait()
     mask_float = mask_ref[...].astype(F32)
-    across = lax.broadcasted_iota(jnp.int32, (tile_cols, pairs), 1) % width
+    column = lax.broadcasted_iota(jnp.int32, (tile_cols, pairs), 1) % width
     mine = (
         lax.broadcasted_iota(jnp.int32, (tile_rows, pairs), 1) // width
         == lax.broadcasted_iota(jnp.int32, (tile_rows, pairs), 0)
@@ -403,7 +409,7 @@
     mask_flat = []
     for chunk in range(CHUNKS):
         spread = (
-            across + chunk * width == lax.broadcasted_iota(jnp.int32, (tile_cols, pairs), 0)
+            column + chunk * width == lax.broadcasted_iota(jnp.int32, (tile_cols, pairs), 0)
         ).astype(F32)
         mask_flat.append(
             jnp.sum(
@@ -419,10 +425,13 @@
         zt_ref[chunk] = jnp.transpose(
             z_ref[:, chunk * width : (chunk + 1) * width, :].astype(F32).reshape(pairs, channels)
         )
-        normed[chunk] = front(0, chunk, zt_ref[chunk], mask_flat[chunk])
-        if chunk == 0:
-            pl.semaphore_wait(barrier, devices - 1)
-        start_k(chunk)
+        normed[chunk] = front(
+            0,
+            chunk,
+            zt_ref[chunk],
+            mask_flat[chunk],
+            lambda target, chunk=chunk: send_k.at[target, chunk],
+        )
     for at in (5, 6, 7, 8):
         loads[at].wait()
     for chunk in range(CHUNKS):
@@ -430,24 +439,24 @@
     spread_inputs(1)
     for layer in range(2):
         spread_outputs(layer)
-    for chunk in range(CHUNKS):
-        wait_k(recv_sem, chunk)
-
-    def panel(ref, chunk, plane, *side):
-        return ref[
-            (chunk, slice(plane * row_count, (plane + 1) * row_count)) + side
-        ].reshape(tokens, lanes)
+    pl.semaphore_wait(barrier, devices - 1)
+    start_k()
+    wait_k(recv_sem)
+
+    def panel(ref, plane, *at):
+        span = (slice(plane * row_count, (plane + 1) * row_count),)
+        return ref[at[:1] + span + at[1:] if ref is not recv_k else span + at].reshape(tokens, lanes)
 
     spans = [(chunk, plane) for chunk in range(CHUNKS) for plane in range(half)]
-    left = jnp.concatenate([panel(recv_k, c, p, 0) for c, p in spans], axis=1)
-    right = jnp.concatenate([panel(recv_k, c, p, 1) for c, p in spans], axis=1)
+    left = jnp.concatenate([panel(recv_k, p, c, 0) for c, p in spans], axis=1)
+    right = jnp.concatenate([panel(recv_k, p, c, 1) for c, p in spans], axis=1)
     lane_group = lane_groups((1, len(spans) * lanes), width) % own
     masks = [(lane_group == k).astype(F32).astype(BF16) for k in range(own)]
     for chunk in range(CHUNKS):
         for c in range(col_count):
             at = (c * CHUNKS + chunk) * width
-            rows = right[at : at + width]
-            stacked = jnp.concatenate([rows * masks[k] for k in range(own)], axis=0)
+            lines = right[at : at + width]
+            stacked = jnp.concatenate([lines * masks[k] for k in range(own)], axis=0)
             product = lax.dot_general(
                 left, stacked, (((1,), (1,)), ((), ())), preferred_element_type=F32
             )
@@ -460,33 +469,57 @@
             chunk, owners : 2 * owners
         ].astype(F32)
         zt_ref[chunk] = back(0, chunk, returned)
-        normed[chunk] = front(1, chunk, zt_ref[chunk], mask_flat[chunk])
+        normed[chunk] = front(
+            1,
+            chunk,
+            zt_ref[chunk],
+            mask_flat[chunk],
+            lambda target, chunk=chunk: send_ab.at[chunk, target],
+        )
         start_ab(chunk)
     for chunk in range(CHUNKS):
         gate(1, chunk, normed[chunk])
+    group = lane_groups((width, lanes), width)
+
+    def pieces(left_chunk, chunk):
+        right = jnp.concatenate([panel(recv_ab, p, chunk, 1) for p in range(half)], axis=1)
+        for mine in range(2):
+            left = jnp.concatenate(
+                [
+                    panel(recv_ab, p, left_chunk, 0) if mine else panel(recv_a, p, left_chunk)
+                    for p in range(half)
+                ],
+                axis=1,
+            )
+            product = contract_first(left, right)
+            base = (near if mine else 1 - near) * half
+            for q in range(half):
+                at = q * lanes
+                for p in range(half):
+                    piece = product[at : at + width, p * lanes : (p + 1) * lanes]
+                    for k in range(1, own):
+                        low = at + k * width
+                        piece = jnp.where(
+                            group == k,
+                            product[low : low + width, p * lanes : (p + 1) * lanes],
+                            piece,
+                        )
+                    send_own[chunk, p, (base + q) * CHUNKS + left_chunk] = piece.astype(BF16)
+
     for chunk in range(CHUNKS):
         wait_ab(recv_sem, chunk)
-
-    left = jnp.concatenate(
-        [panel(recv_a, chunk, c) for c in range(col_count) for chunk in range(CHUNKS)], axis=1
-    )
-    group = lane_groups((width, lanes), width)
-    for chunk in range(CHUNKS):
-        right = jnp.concatenate([panel(recv_b, chunk, p) for p in range(half)], axis=1)
-        product = contract_first(left, right)
-        for p in range(half):
-            for r in range(row_count):
-                at = r * lanes
-                piece = product[at : at + width, p * lanes : (p + 1) * lanes]
-                for k in range(1, own):
-                    low = at + k * width
-                    piece = jnp.where(
-                        group == k,
-                        product[low : low + width, p * lanes : (p + 1) * lanes],
-                        piece,
-                    )
-                send_own[chunk, p, r] = piece.astype(BF16)
+        if chunk < CHUNKS - 1:
+            for other in range(chunk + 1):
+                pieces(chunk, other)
+                if other < chunk:
+                    pieces(other, chunk)
+    last = CHUNKS - 1
+    for chunk in range(last):
+        pieces(last, chunk)
         start_own(chunk)
+    for other in range(CHUNKS):
+        pieces(other, last)
+    start_own(last)
 
     for chunk in range(CHUNKS):
         wait_own(recv_sem, chunk)
@@ -495,10 +528,10 @@
             jnp.transpose(final).reshape(tile_rows, width, channels).astype(BF16)
         )
     for chunk in range(CHUNKS):
-        wait_k(send_sem, chunk)
         wait_sum(send_sem, chunk)
         wait_ab(send_sem, chunk)
         wait_own(send_sem, chunk)
+    wait_k(send_sem)
 
 
 def fused(row_count, col_count, *args):
@@ -526,10 +559,11 @@
             pltpu.VMEM((2, channels, lanes), F32),
             pltpu.VMEM((2, owners, lanes), F32),
             pltpu.VMEM((2, owners, lanes), F32),
-            pltpu.VMEM((2, CHUNKS, owners, 2, tile_rows, lanes), BF16),
+            pltpu.VMEM((owners, CHUNKS, 2, tile_rows, lanes), BF16),
+            pltpu.VMEM((owners, CHUNKS, 2, tile_rows, lanes), BF16),
             pltpu.VMEM((CHUNKS, owners, 2, tile_rows, lanes), BF16),
-            pltpu.VMEM((CHUNKS, devices, tile_rows, lanes), BF16),
             pltpu.VMEM((CHUNKS, owners, tile_rows, lanes), BF16),
+            pltpu.VMEM((CHUNKS, owners, 2, tile_rows, lanes), BF16),
             pltpu.VMEM((CHUNKS, col_count, row_count, tile_rows, lanes), BF16),
             pltpu.VMEM((CHUNKS, devices, tile_rows, lanes), BF16),
             pltpu.VMEM((CHUNKS, half, row_count, tile_rows, lanes), BF16),
@@ -560,6 +594,8 @@
             and tile_rows % 16 == 0
             and tile_rows % own == 0
             and own & (own - 1) == 0
+            and row_count & (row_count - 1) == 0
+            and col_count & (col_count - 1) == 0
             and row_count * tile_rows == col_count * tile_cols
         )
         return fused(row_count, col_count, *args) if fits else on_device(*args)

time: 37.9 us -> 36.1 us (0.953)
  Pallas kernels: 36.2 us -> 34.3 us
    pallas_call x1, Pallas kernels: 36.2 us -> 34.3 us  [fused(): pl.pallas_call(functools.partial(fused_kernel, row_count, col_count), out...]
where the time goes in v2:
time: 36.1 us; the launch traced here: 35.9 us
  Pallas kernels  34.3 us (95%)
  local copies, waits for them, and re-layouts  1.57 us (4%)
    pallas_call x1, Pallas kernels, fused(): pl.pallas_call(functools.partial(fused_kernel, row_count, col_count), out...  34.3 us
    unnamed x1, local copies, waits for them, and re-layouts  1.57 us

profile of v2, /device:TPU:0, one launch (start us, length us, event | category | flops | bytes accessed | tf_op | source)
XLA Modules:
  0.0 35.9 jit_solution(5997676219235733268)
XLA Ops:
  0.0 34.3 %shard_map.91 = bf16[16,32,128]{2,1,0:T(8,128)(2,1)} custom-call(bf16[16,32,128]{2,1,0:T(8,128)(2,1)} %refs_0_.1, s32[16,32]{1,0:T(8,128)} %refs_1_.1, f32[2,128]{1,0:T(2,128)} %refs_2_.1, f32[2,128]{1,0:T(2,128)} %refs_3_.1, bf16[2,128,512]{2,1,0:T(8,128)(2,1)} %refs_4_.1, bf16[2,128,128]{2,1,0:T(8,128)(2,1)} %refs_5_.1, f32[2,128]{1,0:T(2,128)} %refs_6_.1, ...), custom_call_target="tpu_custom_call" | custom-call | tf_op jit(solution)/shard_map/pallas_call | solution.py:547
  34.3 1.6 %copy.11 = bf16[16,32,128]{2,1,0:T(8,128)(2,1)} copy(bf16[16,32,128]{2,1,0:T(8,128)(2,1)} %shard_map.91) | data formatting | bytes 262144

commit v3 on v2

--- a/solution.py
+++ b/solution.py
@@ -177,6 +177,8 @@
     zt_ref,
     tmp_ref,
     gated_ref,
+    projt_ref,
+    outwt_ref,
     in_gain_ref,
     in_bias_ref,
     gain_ref,
@@ -237,7 +239,8 @@
     def greet(trow, tcol):
         pl.semaphore_signal(barrier, inc=1, device_id=(trow, tcol), device_id_type=MESH)
 
-    each(greet, across + within)
+    greet(row, cols[half])
+    each(greet, within)
 
     def send(source, target, at, trow, tcol):
         pltpu.make_async_remote_copy(
@@ -282,7 +285,7 @@
         slots = recv_sum.at[chunk, pl.ds(0, devices - 1)]
         pltpu.make_async_copy(slots, slots, sem.at[CHUNKS + chunk]).wait()
 
-    def start_ab(chunk):
+    def start_a(chunk):
         each(
             lambda trow, tcol: send(
                 send_ab.at[chunk, owner(trow, tcol), 0],
@@ -293,6 +296,8 @@
             ),
             across,
         )
+
+    def start_ab(chunk):
         each(
             lambda trow, tcol: send(
                 send_ab.at[chunk, owner(trow, tcol)],
@@ -341,20 +346,21 @@
                 packed = jnp.where(group == k, wide[k * owners : (k + 1) * owners], packed)
             kept[layer] = packed
 
-    def front(layer, chunk, current, mask_flat, target_at):
+    def front(layer, current, mask_flat, target_at, sent=None):
         centred = current - jnp.mean(current, axis=0, keepdims=True)
         scale = lax.rsqrt(jnp.mean(centred * centred, axis=0, keepdims=True) + epsilon)
         gain = jnp.concatenate([in_gain_ref[layer]] * blocks, axis=1)
         bias = jnp.concatenate([in_bias_ref[layer]] * blocks, axis=1)
         normed = (centred * scale * gain + bias).astype(BF16)
-        projected = contract_first(proj_ref[layer], normed)
         for side in range(2):
             first = 2 * side * hidden
-            panel = (
-                sigmoid(projected[first : first + hidden])
-                * projected[first + hidden : first + 2 * hidden]
-                * mask_flat
-            )
+            if layer == 0:
+                weights = proj_ref[layer, :, first : first + 2 * hidden]
+                projected = contract_first(weights, normed)
+            else:
+                weights = projt_ref[first : first + 2 * hidden]
+                projected = jnp.dot(weights, normed, preferred_element_type=F32)
+            panel = sigmoid(projected[:hidden]) * projected[hidden:] * mask_flat
             for block in range(blocks):
                 parts = [
                     panel[k * owners : (k + 1) * owners, block * lanes : (block + 1) * lanes]
@@ -367,6 +373,8 @@
                 target_at(target)[side] = tmp_ref[
                     side, pl.ds(target, tile_rows, stride=owners), :
                 ].astype(BF16)
+            if sent is not None:
+                sent[side]()
         return normed
 
     def gate(layer, chunk, normed):
@@ -393,7 +401,9 @@
                 tmp_ref[0, pl.ds(block * own + q, owners, stride=tile_rows), :] for q in range(own)
             ]
             wide_blocks.append(jnp.concatenate(swap_groups(parts, width), axis=0).astype(BF16))
-        update = contract_first(outw_ref[layer], jnp.concatenate(wide_blocks, axis=1))
+        update = jnp.dot(
+            outwt_ref[layer], jnp.concatenate(wide_blocks, axis=1), preferred_element_type=F32
+        )
         return zt_ref[chunk] + gated_ref[chunk] * update
 
     for at in (2, 3):
@@ -427,20 +437,23 @@
         )
         normed[chunk] = front(
             0,
-            chunk,
             zt_ref[chunk],
             mask_flat[chunk],
             lambda target, chunk=chunk: send_k.at[target, chunk],
         )
+    pl.semaphore_wait(barrier, owners)
+    start_k()
     for at in (5, 6, 7, 8):
         loads[at].wait()
+    for layer in range(1, 2):
+        projt_ref[...] = jnp.transpose(proj_ref[layer])
+    for layer in range(2):
+        outwt_ref[layer] = jnp.transpose(outw_ref[layer])
     for chunk in range(CHUNKS):
         gate(0, chunk, normed[chunk])
     spread_inputs(1)
     for layer in range(2):
         spread_outputs(layer)
-    pl.semaphore_wait(barrier, devices - 1)
-    start_k()
     wait_k(recv_sem)
 
     def panel(ref, plane, *at):
@@ -471,12 +484,11 @@
         zt_ref[chunk] = back(0, chunk, returned)
         normed[chunk] = front(
             1,
-            chunk,
             zt_ref[chunk],
             mask_flat[chunk],
             lambda target, chunk=chunk: send_ab.at[chunk, target],
-        )
-        start_ab(chunk)
+            (lambda chunk=chunk: start_a(chunk), lambda chunk=chunk: start_ab(chunk)),
+        )
     for chunk in range(CHUNKS):
         gate(1, chunk, normed[chunk])
     group = lane_groups((width, lanes), width)
@@ -555,6 +567,8 @@
             pltpu.VMEM((CHUNKS, channels, pairs), F32),
             pltpu.VMEM((2, tile_rows * owners, lanes), F32),
             pltpu.VMEM((CHUNKS, channels, pairs), F32),
+            pltpu.VMEM(args[4].shape[:0:-1], BF16),
+            pltpu.VMEM(args[8].shape[:1] + args[8].shape[:0:-1], BF16),
             pltpu.VMEM((2, channels, lanes), F32),
             pltpu.VMEM((2, channels, lanes), F32),
             pltpu.VMEM((2, owners, lanes), F32),
@@ -571,8 +585,10 @@
             pltpu.SemaphoreType.DMA((5 * CHUNKS,)),
             pltpu.SemaphoreType.DMA((5 * CHUNKS,)),
         ],
-        compiler_params=pltpu.CompilerParams(collective_id=0, has_side_effects=True),
-    )(*args)
+        compiler_params=pltpu.CompilerParams(
+            collective_id=0, has_side_effects=True, vmem_limit_bytes=16 << 20
+        ),
+    )(*[pltpu.with_memory_space_constraint(arg, pltpu.HBM) for arg in args])
 
 
 def solution(mesh):

time: 36.1 us -> 33 us (0.914)
  Pallas kernels: 34.3 us -> 32.2 us
  local copies, waits for them, and re-layouts: 1.57 us -> 0.66 us
    pallas_call x1, Pallas kernels: 34.3 us -> 32.2 us  [fused(): pl.pallas_call(functools.partial(fused_kernel, row_count, col_count), out...]
    unnamed x1, local copies, waits for them, and re-layouts: 1.57 us -> 0.66 us
where the time goes in v3:
time: 33 us; the launch traced here: 32.8 us
  Pallas kernels  32.2 us (98%)
  local copies, waits for them, and re-layouts  0.66 us (2%)
    pallas_call x1, Pallas kernels, fused(): pl.pallas_call(functools.partial(fused_kernel, row_count, col_count), out...  32.2 us

profile of v3, /device:TPU:0, one launch (start us, length us, event | category | flops | bytes accessed | tf_op | source)
XLA Modules:
  0.0 32.8 jit_solution(8084146047392246291)
XLA Ops:
  0.0 32.2 %shard_map.91 = bf16[16,32,128]{2,1,0:T(8,128)(2,1)S(1)} custom-call(bf16[16,32,128]{2,1,0:T(8,128)(2,1)} %refs_0_.1, s32[16,32]{1,0:T(8,128)} %refs_1_.1, f32[2,128]{1,0:T(2,128)} %refs_2_.1, f32[2,128]{1,0:T(2,128)} %refs_3_.1, bf16[2,128,512]{2,1,0:T(8,128)(2,1)} %refs_4_.1, bf16[2,128,128]{2,1,0:T(8,128)(2,1)} %refs_5_.1, f32[2,128]{1,0:T(2,128)} %refs_6_.1, ...), custom_call_target="tpu_custom_call" | custom-call | tf_op jit(solution)/shard_map/pallas_call | solution.py:559
  32.2 0.7 %copy.11 = bf16[16,32,128]{2,1,0:T(8,128)(2,1)} copy(bf16[16,32,128]{2,1,0:T(8,128)(2,1)S(1)} %shard_map.91) | data formatting | bytes 262144

commit v4 on v3

--- a/solution.py
+++ b/solution.py
@@ -123,21 +123,18 @@
 
 def swap_groups(blocks, width):
     count = len(blocks)
-    blocks = list(blocks)
     lanes = count * width
     group = lane_groups(blocks[0].shape, width)
-    step = count // 2
-    while step:
-        low = (group // step) % 2 == 0
-        for p in range(count):
-            if p & step:
-                continue
-            first, second = blocks[p], blocks[p + step]
-            shift = step * width
-            blocks[p] = jnp.where(low, first, pltpu.roll(second, shift, 1))
-            blocks[p + step] = jnp.where(low, pltpu.roll(first, lanes - shift, 1), second)
-        step //= 2
-    return blocks
+    held = [pltpu.roll(part, at * width, 1) if at else part for at, part in enumerate(blocks)]
+    step = 1
+    while step < count:
+        high = (group // step) % 2 == 1
+        held = [jnp.where(high, held[(at + step) % count], held[at]) for at in range(count)]
+        step *= 2
+    return [
+        pltpu.roll(held[-at % count], lanes - at * width, 1) if at else held[0]
+        for at in range(count)
+    ]
 
 
 def columns_of(row_vector, lanes):
@@ -316,22 +313,18 @@
         slots = recv_ab.at[chunk, pl.ds(0, owners - 1)]
         pltpu.make_async_copy(slots, slots, sem.at[3 * CHUNKS + chunk]).wait()
 
-    def start_own(chunk):
+    def start_own():
         each(
             lambda trow, tcol: send(
-                send_own.at[chunk, lax.rem(tcol, half), trow],
-                recv_own.at[chunk, me],
-                4 * CHUNKS + chunk,
-                trow,
-                tcol,
+                send_own.at[lax.rem(tcol, half), trow], recv_own.at[me], 4 * CHUNKS, trow, tcol
             ),
             within,
         )
-        recv_own[chunk, me] = send_own[chunk, inner, row]
-
-    def wait_own(sem, chunk):
-        slots = recv_own.at[chunk, pl.ds(0, owners - 1)]
-        pltpu.make_async_copy(slots, slots, sem.at[4 * CHUNKS + chunk]).wait()
+        recv_own[me] = send_own[inner, row]
+
+    def wait_own(sem):
+        slots = recv_own.at[pl.ds(0, owners - 1)]
+        pltpu.make_async_copy(slots, slots, sem.at[4 * CHUNKS]).wait()
 
     def spread_inputs(layer):
         in_gain_ref[layer] = columns_of(in_gain[layer : layer + 1, :], lanes)
@@ -360,7 +353,7 @@
             else:
                 weights = projt_ref[first : first + 2 * hidden]
                 projected = jnp.dot(weights, normed, preferred_element_type=F32)
-            panel = sigmoid(projected[:hidden]) * projected[hidden:] * mask_flat
+            panel = (sigmoid(projected[:hidden]) * projected[hidden:] * mask_flat).astype(BF16)
             for block in range(blocks):
                 parts = [
                     panel[k * owners : (k + 1) * owners, block * lanes : (block + 1) * lanes]
@@ -368,7 +361,7 @@
                 ]
                 for q, part in enumerate(swap_groups(parts, width)):
                     line = block * own + q
-                    tmp_ref[side, line * owners : (line + 1) * owners, :] = part
+                    tmp_ref[side, line * owners : (line + 1) * owners, :] = part.astype(F32)
             for target in range(owners):
                 target_at(target)[side] = tmp_ref[
                     side, pl.ds(target, tile_rows, stride=owners), :
@@ -392,13 +385,13 @@
         centred = returned - over_channels(returned)[None]
         scale = lax.rsqrt(over_channels(centred * centred) + epsilon)
         for d in range(owners):
-            tmp_ref[0, d * tile_rows : (d + 1) * tile_rows, :] = (
+            tmp_ref[chunk, d * tile_rows : (d + 1) * tile_rows, :] = (
                 centred[d] * scale * gain_ref[layer, d : d + 1, :] + bias_ref[layer, d : d + 1, :]
             )
         wide_blocks = []
         for block in range(blocks):
             parts = [
-                tmp_ref[0, pl.ds(block * own + q, owners, stride=tile_rows), :] for q in range(own)
+                tmp_ref[chunk, pl.ds(block * own + q, owners, stride=tile_rows), :] for q in range(own)
             ]
             wide_blocks.append(jnp.concatenate(swap_groups(parts, width), axis=0).astype(BF16))
         update = jnp.dot(
@@ -516,7 +509,7 @@
                             product[low : low + width, p * lanes : (p + 1) * lanes],
                             piece,
                         )
-                    send_own[chunk, p, (base + q) * CHUNKS + left_chunk] = piece.astype(BF16)
+                    send_own[p, (base + q) * CHUNKS + left_chunk, chunk] = piece.astype(BF16)
 
     for chunk in range(CHUNKS):
         wait_ab(recv_sem, chunk)
@@ -528,21 +521,20 @@
     last = CHUNKS - 1
     for chunk in range(last):
         pieces(last, chunk)
-        start_own(chunk)
     for other in range(CHUNKS):
         pieces(other, last)
-    start_own(last)
-
-    for chunk in range(CHUNKS):
-        wait_own(recv_sem, chunk)
-        final = back(1, chunk, recv_own[chunk].astype(F32))
+    start_own()
+
+    wait_own(recv_sem)
+    for chunk in range(CHUNKS):
+        final = back(1, chunk, recv_own[:, chunk].astype(F32))
         out_ref[:, chunk * width : (chunk + 1) * width, :] = (
             jnp.transpose(final).reshape(tile_rows, width, channels).astype(BF16)
         )
     for chunk in range(CHUNKS):
         wait_sum(send_sem, chunk)
         wait_ab(send_sem, chunk)
-        wait_own(send_sem, chunk)
+    wait_own(send_sem)
     wait_k(send_sem)
 
 
@@ -580,8 +572,8 @@
             pltpu.VMEM((CHUNKS, owners, 2, tile_rows, lanes), BF16),
             pltpu.VMEM((CHUNKS, col_count, row_count, tile_rows, lanes), BF16),
             pltpu.VMEM((CHUNKS, devices, tile_rows, lanes), BF16),
-            pltpu.VMEM((CHUNKS, half, row_count, tile_rows, lanes), BF16),
-            pltpu.VMEM((CHUNKS, owners, tile_rows, lanes), BF16),
+            pltpu.VMEM((half, row_count, CHUNKS, tile_rows, lanes), BF16),
+            pltpu.VMEM((owners, CHUNKS, tile_rows, lanes), BF16),
             pltpu.SemaphoreType.DMA((5 * CHUNKS,)),
             pltpu.SemaphoreType.DMA((5 * CHUNKS,)),
         ],

time: 33 us -> 32.1 us (0.973)
  Pallas kernels: 32.2 us -> 31.3 us
    pallas_call x1, Pallas kernels: 32.2 us -> 31.3 us  [fused(): pl.pallas_call(functools.partial(fused_kernel, row_count, col_count), out...]
where the time goes in v4:
time: 32.1 us; the launch traced here: 31.9 us
  Pallas kernels  31.3 us (98%)
  local copies, waits for them, and re-layouts  0.66 us (2%)
    pallas_call x1, Pallas kernels, fused(): pl.pallas_call(functools.partial(fused_kernel, row_count, col_count), out...  31.3 us
    unnamed x1, local copies, waits for them, and re-layouts  0.66 us

profile of v4, /device:TPU:0, one launch (start us, length us, event | category | flops | bytes accessed | tf_op | source)
XLA Modules:
  0.0 31.9 jit_solution(7939736719428192264)
XLA Ops:
  0.0 31.3 %shard_map.91 = bf16[16,32,128]{2,1,0:T(8,128)(2,1)S(1)} custom-call(bf16[16,32,128]{2,1,0:T(8,128)(2,1)} %refs_0_.1, s32[16,32]{1,0:T(8,128)} %refs_1_.1, f32[2,128]{1,0:T(2,128)} %refs_2_.1, f32[2,128]{1,0:T(2,128)} %refs_3_.1, bf16[2,128,512]{2,1,0:T(8,128)(2,1)} %refs_4_.1, bf16[2,128,128]{2,1,0:T(8,128)(2,1)} %refs_5_.1, f32[2,128]{1,0:T(2,128)} %refs_6_.1, ...), custom_call_target="tpu_custom_call" | custom-call | tf_op jit(solution)/shard_map/pallas_call | solution.py:551
  31.3 0.7 %copy.11 = bf16[16,32,128]{2,1,0:T(8,128)(2,1)} copy(bf16[16,32,128]{2,1,0:T(8,128)(2,1)S(1)} %shard_map.91) | data formatting | bytes 262144

commit v5 on v4

--- a/solution.py
+++ b/solution.py
@@ -274,7 +274,7 @@
                 trow,
                 tcol,
             ),
-            across + within,
+            (within + across if chunk else across + within),
         )
         recv_sum[chunk, near * owners + me] = send_sum[chunk, col, row]
 
@@ -291,7 +291,7 @@
                 trow,
                 tcol,
             ),
-            across,
+            across[::-1] if chunk else across,
         )
 
     def start_ab(chunk):

time: 32.1 us -> 31.6 us (0.984)
  Pallas kernels: 31.3 us -> 30.8 us
    pallas_call x1, Pallas kernels: 31.3 us -> 30.8 us  [fused(): pl.pallas_call(functools.partial(fused_kernel, row_count, col_count), out...]
where the time goes in v5:
time: 31.6 us; the launch traced here: 31.5 us
  Pallas kernels  30.8 us (97%)
  local copies, waits for them, and re-layouts  0.66 us (2%)
    pallas_call x1, Pallas kernels, fused(): pl.pallas_call(functools.partial(fused_kernel, row_count, col_count), out...  30.8 us
    unnamed x1, local copies, waits for them, and re-layouts  0.66 us

profile of v5, /device:TPU:0, one launch (start us, length us, event | category | flops | bytes accessed | tf_op | source)
XLA Modules:
  0.0 31.5 jit_solution(6693878530494097891)
XLA Ops:
  0.0 30.8 %shard_map.91 = bf16[16,32,128]{2,1,0:T(8,128)(2,1)S(1)} custom-call(bf16[16,32,128]{2,1,0:T(8,128)(2,1)} %refs_0_.1, s32[16,32]{1,0:T(8,128)} %refs_1_.1, f32[2,128]{1,0:T(2,128)} %refs_2_.1, f32[2,128]{1,0:T(2,128)} %refs_3_.1, bf16[2,128,512]{2,1,0:T(8,128)(2,1)} %refs_4_.1, bf16[2,128,128]{2,1,0:T(8,128)(2,1)} %refs_5_.1, f32[2,128]{1,0:T(2,128)} %refs_6_.1, ...), custom_call_target="tpu_custom_call" | custom-call | tf_op jit(solution)/shard_map/pallas_call | solution.py:551
  30.8 0.7 %copy.11 = bf16[16,32,128]{2,1,0:T(8,128)(2,1)} copy(bf16[16,32,128]{2,1,0:T(8,128)(2,1)S(1)} %shard_map.91) | data formatting | bytes 262144

commit v6 on v5

--- a/solution.py
+++ b/solution.py
@@ -174,6 +174,8 @@
     zt_ref,
     tmp_ref,
     gated_ref,
+    flat_ref,
+    gated_flat_ref,
     projt_ref,
     outwt_ref,
     in_gain_ref,
@@ -394,9 +396,10 @@
                 tmp_ref[chunk, pl.ds(block * own + q, owners, stride=tile_rows), :] for q in range(own)
             ]
             wide_blocks.append(jnp.concatenate(swap_groups(parts, width), axis=0).astype(BF16))
-        update = jnp.dot(
-            outwt_ref[layer], jnp.concatenate(wide_blocks, axis=1), preferred_element_type=F32
-        )
+        wide = jnp.concatenate(wide_blocks, axis=1)
+        if layer == 1:
+            return flat_ref[chunk] + gated_flat_ref[chunk] * contract_first(wide, outw_ref[layer])
+        update = jnp.dot(outwt_ref[layer], wide, preferred_element_type=F32)
         return zt_ref[chunk] + gated_ref[chunk] * update
 
     for at in (2, 3):
@@ -454,11 +457,12 @@
         return ref[at[:1] + span + at[1:] if ref is not recv_k else span + at].reshape(tokens, lanes)
 
     spans = [(chunk, plane) for chunk in range(CHUNKS) for plane in range(half)]
-    left = jnp.concatenate([panel(recv_k, p, c, 0) for c, p in spans], axis=1)
-    right = jnp.concatenate([panel(recv_k, p, c, 1) for c, p in spans], axis=1)
     lane_group = lane_groups((1, len(spans) * lanes), width) % own
-    masks = [(lane_group == k).astype(F32).astype(BF16) for k in range(own)]
-    for chunk in range(CHUNKS):
+
+    def sums(chunk):
+        left = jnp.concatenate([panel(recv_k, p, c, 0) for c, p in spans], axis=1)
+        right = jnp.concatenate([panel(recv_k, p, c, 1) for c, p in spans], axis=1)
+        masks = [(lane_group == k).astype(F32).astype(BF16) for k in range(own)]
         for c in range(col_count):
             at = (c * CHUNKS + chunk) * width
             lines = right[at : at + width]
@@ -468,6 +472,10 @@
             )
             send_sum[chunk, c] = product.astype(BF16).reshape(row_count, tile_rows, lanes)
         start_sum(chunk)
+
+    sums(0)
+    for chunk in range(1, CHUNKS):
+        pl.when(row >= 0)(lambda chunk=chunk: sums(chunk))
 
     for chunk in range(CHUNKS):
         wait_sum(recv_sem, chunk)
@@ -480,10 +488,15 @@
             zt_ref[chunk],
             mask_flat[chunk],
             lambda target, chunk=chunk: send_ab.at[chunk, target],
-            (lambda chunk=chunk: start_a(chunk), lambda chunk=chunk: start_ab(chunk)),
-        )
-    for chunk in range(CHUNKS):
-        gate(1, chunk, normed[chunk])
+            (
+                (lambda chunk=chunk: start_a(chunk), lambda chunk=chunk: start_ab(chunk))
+                if chunk < CHUNKS - 1
+                else (lambda: None, lambda chunk=chunk: (start_a(chunk), start_ab(chunk)))
+            ),
+        )
+    for chunk in range(CHUNKS):
+        gated_flat_ref[chunk] = sigmoid(contract_first(normed[chunk], gate_ref[1]))
+        flat_ref[chunk] = jnp.transpose(zt_ref[chunk])
     group = lane_groups((width, lanes), width)
 
     def pieces(left_chunk, chunk):
@@ -529,7 +542,7 @@
     for chunk in range(CHUNKS):
         final = back(1, chunk, recv_own[:, chunk].astype(F32))
         out_ref[:, chunk * width : (chunk + 1) * width, :] = (
-            jnp.transpose(final).reshape(tile_rows, width, channels).astype(BF16)
+            final.reshape(tile_rows, width, channels).astype(BF16)
         )
     for chunk in range(CHUNKS):
         wait_sum(send_sem, chunk)
@@ -559,6 +572,8 @@
             pltpu.VMEM((CHUNKS, channels, pairs), F32),
             pltpu.VMEM((2, tile_rows * owners, lanes), F32),
             pltpu.VMEM((CHUNKS, channels, pairs), F32),
+            pltpu.VMEM((CHUNKS, pairs, channels), F32),
+            pltpu.VMEM((CHUNKS, pairs, channels), F32),
             pltpu.VMEM(args[4].shape[:0:-1], BF16),
             pltpu.VMEM(args[8].shape[:1] + args[8].shape[:0:-1], BF16),
             pltpu.VMEM((2, channels, lanes), F32),

time: 31.6 us -> 31.5 us (level)
  no operation moved by 1% of the time
where the time goes in v6:
time: 31.5 us; the launch traced here: 31.4 us
  Pallas kernels  30.7 us (97%)
  local copies, waits for them, and re-layouts  0.66 us (2%)
    pallas_call x1, Pallas kernels, fused(): pl.pallas_call(functools.partial(fused_kernel, row_count, col_count), out...  30.7 us
    unnamed x1, local copies, waits for them, and re-layouts  0.66 us

profile of v6, /device:TPU:0, one launch (start us, length us, event | category | flops | bytes accessed | tf_op | source)
XLA Modules:
  0.0 31.4 jit_solution(12919706832934356464)
XLA Ops:
  0.0 30.7 %shard_map.91 = bf16[16,32,128]{2,1,0:T(8,128)(2,1)S(1)} custom-call(bf16[16,32,128]{2,1,0:T(8,128)(2,1)} %refs_0_.1, s32[16,32]{1,0:T(8,128)} %refs_1_.1, f32[2,128]{1,0:T(2,128)} %refs_2_.1, f32[2,128]{1,0:T(2,128)} %refs_3_.1, bf16[2,128,512]{2,1,0:T(8,128)(2,1)} %refs_4_.1, bf16[2,128,128]{2,1,0:T(8,128)(2,1)} %refs_5_.1, f32[2,128]{1,0:T(2,128)} %refs_6_.1, ...), custom_call_target="tpu_custom_call" | custom-call | tf_op jit(solution)/shard_map/pallas_call | solution.py:564
  30.7 0.7 %copy.11 = bf16[16,32,128]{2,1,0:T(8,128)(2,1)} copy(bf16[16,32,128]{2,1,0:T(8,128)(2,1)S(1)} %shard_map.91) | data formatting | bytes 262144

commit v7 on v6

--- a/solution.py
+++ b/solution.py
@@ -238,8 +238,8 @@
     def greet(trow, tcol):
         pl.semaphore_signal(barrier, inc=1, device_id=(trow, tcol), device_id_type=MESH)
 
+    each(greet, within)
     greet(row, cols[half])
-    each(greet, within)
 
     def send(source, target, at, trow, tcol):
         pltpu.make_async_remote_copy(

time: 31.5 us -> 31.5 us (level)
  no operation moved by 1% of the time
where the time goes in v7:
time: 31.5 us; the launch traced here: 31.4 us
  Pallas kernels  30.7 us (97%)
  local copies, waits for them, and re-layouts  0.66 us (2%)
    pallas_call x1, Pallas kernels, fused(): pl.pallas_call(functools.partial(fused_kernel, row_count, col_count), out...  30.7 us
    unnamed x1, local copies, waits for them, and re-layouts  0.66 us

profile of v7, /device:TPU:0, one launch (start us, length us, event | category | flops | bytes accessed | tf_op | source)
XLA Modules:
  0.0 31.4 jit_solution(13781355791686205247)
XLA Ops:
  0.0 30.7 %shard_map.91 = bf16[16,32,128]{2,1,0:T(8,128)(2,1)S(1)} custom-call(bf16[16,32,128]{2,1,0:T(8,128)(2,1)} %refs_0_.1, s32[16,32]{1,0:T(8,128)} %refs_1_.1, f32[2,128]{1,0:T(2,128)} %refs_2_.1, f32[2,128]{1,0:T(2,128)} %refs_3_.1, bf16[2,128,512]{2,1,0:T(8,128)(2,1)} %refs_4_.1, bf16[2,128,128]{2,1,0:T(8,128)(2,1)} %refs_5_.1, f32[2,128]{1,0:T(2,128)} %refs_6_.1, ...), custom_call_target="tpu_custom_call" | custom-call | tf_op jit(solution)/shard_map/pallas_call | solution.py:564
  30.7 0.7 %copy.11 = bf16[16,32,128]{2,1,0:T(8,128)(2,1)} copy(bf16[16,32,128]{2,1,0:T(8,128)(2,1)S(1)} %shard_map.91) | data formatting | bytes 262144
